TPU v7x, 32 devices: a whole 2x2x4 slice. The times are simulated.
32 devices in a mesh: dp: 16 (over z, x, core), tensor: 2 (over y).
Axes of the slice: x: 2, y: 2, z: 4, core: 2. Of those that a mesh axis runs over, the one named last changes fastest.
Arguments:
- hidden_in: bfloat16 [4096, 1152], P('dp'), may hold values from -6 to 6
- condition: bfloat16 [112, 1152], P('dp'), may hold values from -6 to 6
- heights: int32 [16, 7], P('dp'), may hold values from 3 to 6, as said below
- widths: int32 [16, 7], P('dp'), may hold values from 3 to 6, as said below
- ada_weight: bfloat16 [1152, 6912], P('dp', 'tensor'), may hold values from -0.1875 to 0.1875
- attn_weight: bfloat16 [1152, 4, 1152], P('dp', None, 'tensor'), may hold values from -0.1875 to 0.1875
- forget_weight: bfloat16 [1152, 16], P('dp', 'tensor'), may hold values from -0.1875 to 0.1875
- forget_bias: float32 [16], P('tensor'), may hold values from -4 to 3
- conv_weight: bfloat16 [9, 1152], P(None, 'tensor'), may hold values from -1.796875 to 1.796875
- out_weight: bfloat16 [1152, 1152], P('tensor', 'dp'), may hold values from -0.1875 to 0.1875
- up_weight: bfloat16 [1152, 4608], P('dp', 'tensor'), may hold values from -0.1875 to 0.1875
- down_weight: bfloat16 [4608, 1152], P('tensor', 'dp'), may hold values from -0.09375 to 0.09375
- cotangent: bfloat16 [4096, 1152], P('dp'), may hold values from -6 to 6
Outputs:
- hidden_out: bfloat16 [4096, 1152], P('dp')
- grad_hidden: bfloat16 [4096, 1152], P('dp')
- grad_condition: bfloat16 [112, 1152], P('dp')
- grad_ada: float32 [1152, 6912], P('dp', 'tensor')
- grad_attn: float32 [1152, 4, 1152], P('dp', None, 'tensor')
- grad_forget: float32 [1152, 16], P('dp', 'tensor')
- grad_bias: float32 [16], P('tensor')
- grad_conv: float32 [9, 1152], P(None, 'tensor')
- grad_out_weight: float32 [1152, 1152], P('tensor', 'dp')
- grad_up: float32 [1152, 4608], P('dp', 'tensor')
- grad_down: float32 [4608, 1152], P('tensor', 'dp')
Inputs may be any that keep to these rules, and one draw needn't show every extreme that they name: `heights`: each packed sequence holds 7 images laid back to back from its first slot; the slots after them are empty. `widths`: as for heights.
All inputs are finite; a program needn't handle non-finite values.
Results may differ from a plain program's by a relative error of at most 0.011.
Values may be sent and summed in bfloat16 or wider, within the bound.
A program may use at most 256 MiB of HBM per device.

v0:
```python
import functools
import jax
import jax.numpy as jnp
from jax import lax
from jax.sharding import PartitionSpec as P

BLOCK = 64
gate_norm = 16.0
norm_epsilon = 1e-06
head_epsilon = 1e-05
highest_precision = lax.Precision.HIGHEST


def layout(heights, widths, length):
    sequence_count, number_of_images = heights.shape
    image_area = heights * widths
    image_ends = jnp.cumsum(image_area, axis=1)
    starts = image_ends - image_area
    position = jnp.arange(length, dtype=jnp.int32)
    segment = jnp.sum((position[None, :, None] >= image_ends[:, None, :]).astype(jnp.int32), axis=2)
    choose_rows = (
        segment[:, :, None] == jnp.arange(number_of_images, dtype=jnp.int32)[None, None, :]
    )
    zero_int = jnp.zeros((), jnp.int32)
    start_at = jnp.sum(jnp.where(choose_rows, starts[:, None, :], zero_int), axis=2)
    image_width = jnp.maximum(
        jnp.sum(jnp.where(choose_rows, widths[:, None, :], zero_int), axis=2), 1
    )
    image_height = jnp.sum(jnp.where(choose_rows, heights[:, None, :], zero_int), axis=2)
    offset_in = position[None, :] - start_at
    row_index = offset_in // image_width
    col_index = offset_in - row_index * image_width
    is_valid = segment < number_of_images
    seq_base = jnp.arange(sequence_count, dtype=jnp.int32)[:, None]
    token_keys = (segment + seq_base * (number_of_images + 1)).reshape(-1)
    tap_list = []
    for vertical in (-1, 0, 1):
        for lateral in (-1, 0, 1):
            inside = (
                is_valid
                & (row_index + vertical >= 0)
                & (row_index + vertical < image_height)
                & (col_index + lateral >= 0)
                & (col_index + lateral < image_width)
            )
            target = (
                jnp.clip(position[None, :] + vertical * image_width + lateral, 0, length - 1)
                + seq_base * length
            )
            tap_list.append((target.reshape(-1), inside.reshape(-1).astype(jnp.float32)))
    return (choose_rows.astype(jnp.float32), token_keys, tap_list)


def modulate(values, shift, scale):
    centre = values - jnp.mean(values, axis=1, keepdims=True)
    spread = jnp.mean(centre * centre, axis=1, keepdims=True)
    return centre * lax.rsqrt(spread + norm_epsilon) * (1.0 + scale) + shift


def gelu_tanh(values):
    return jax.nn.gelu(values, approximate=True)


def tensor_total(partial_terms):
    summed_half = lax.psum_scatter(partial_terms, "tensor", scatter_dimension=1, tiled=True)
    return lax.all_gather(summed_half, "tensor", axis=1, tiled=True)


def token_mixer(queries, keys_in, values, gate_raw, forget_raw, conv_kernel, token_keys, tap_list):
    number_of_tokens, channels = queries.shape
    head_count = forget_raw.shape[1]
    head_size = channels // head_count
    block_count = number_of_tokens // BLOCK
    log_decay = jax.nn.log_sigmoid(forget_raw) / gate_norm
    cumulative = jnp.cumsum(log_decay.reshape(block_count, BLOCK, head_count), axis=1)
    decay_rows = jnp.transpose(cumulative, (0, 2, 1))
    query_blocks = (jax.nn.elu(queries) + 1.0).reshape(block_count, BLOCK, head_count, head_size)
    key_blocks = (jax.nn.elu(keys_in) + 1.0).reshape(block_count, BLOCK, head_count, head_size)
    value_blocks = values.reshape(block_count, BLOCK, head_count, head_size)
    block_keys = token_keys.reshape(block_count, BLOCK)
    position = jnp.arange(BLOCK, dtype=jnp.int32)
    lower = position[:, None] >= position[None, :]
    same_heads = ((block_keys[:, :, None] == block_keys[:, None, :]) & lower[None, :, :])[
        :, None, :, :
    ]
    exponent = decay_rows[:, :, :, None] - decay_rows[:, :, None, :]
    decays = jnp.where(same_heads, jnp.exp(jnp.where(same_heads, exponent, 0.0)), 0.0)
    scores = jnp.einsum("bthk,bshk->bhts", query_blocks, key_blocks, precision=highest_precision)
    inside_part = jnp.einsum(
        "bhts,bshk->bthk", scores * decays, value_blocks, precision=highest_precision
    )
    last_decay = decay_rows[:, :, -1]
    last_key = block_keys[:, -1]
    member = (block_keys == last_key[:, None]).astype(jnp.float32)
    end_weight = member[:, :, None] * jnp.exp(last_decay[:, None, :] - cumulative)
    weighted = key_blocks * end_weight[:, :, :, None]
    summary = jnp.einsum("bshk,bshj->bhkj", weighted, value_blocks, precision=highest_precision)
    prior_key = jnp.concatenate([jnp.full((1,), -1, jnp.int32), last_key[:-1]])
    keep_state = (last_key == prior_key).astype(jnp.float32)
    factor = keep_state[:, None] * jnp.exp(last_decay)

    def advance(carry_state, inputs):
        scale_now, added = inputs
        return (scale_now[:, None, None] * carry_state + added, carry_state)

    initial = jnp.zeros((head_count, head_size, head_size), jnp.float32)
    final_state, start_states = lax.scan(advance, initial, (factor, summary))
    carries = (block_keys == prior_key[:, None]).astype(jnp.float32)
    lifted = query_blocks * jnp.exp(cumulative)[:, :, :, None] * carries[:, :, None, None]
    carried_part = jnp.einsum("bthk,bhkj->bthj", lifted, start_states, precision=highest_precision)
    attended = (inside_part + carried_part).reshape(number_of_tokens, head_count, head_size)
    normed = attended * lax.rsqrt(
        jnp.mean(attended * attended, axis=2, keepdims=True) + head_epsilon
    )
    gated_out = normed.reshape(number_of_tokens, channels) * jax.nn.silu(gate_raw)
    spatial = jnp.zeros_like(gated_out)
    for tap_number, (target, inside) in enumerate(tap_list):
        spatial = (
            spatial
            + conv_kernel[tap_number][None, :]
            * jnp.take(gated_out, target, axis=0)
            * inside[:, None]
        )
    return gated_out + spatial


def body(
    hidden_in,
    condition,
    heights,
    widths,
    ada_weight,
    attn_weight,
    forget_weight,
    forget_bias,
    conv_weight,
    out_weight,
    up_weight,
    down_weight,
    cotangent,
):
    sequence_count, number_of_images = heights.shape
    number_of_tokens, hidden_width = hidden_in.shape
    length = number_of_tokens // sequence_count
    half_width = conv_weight.shape[1]
    choose_rows, token_keys, tap_list = layout(heights, widths, length)
    shards = (ada_weight, attn_weight, forget_weight, out_weight, up_weight, down_weight)
    full_ada, full_attn, full_forget, full_out, full_up, full_down = (
        lax.all_gather(ada_weight, "dp", axis=0, tiled=True),
        lax.all_gather(attn_weight, "dp", axis=0, tiled=True),
        lax.all_gather(forget_weight, "dp", axis=0, tiled=True),
        lax.all_gather(out_weight, "dp", axis=1, tiled=True),
        lax.all_gather(up_weight, "dp", axis=0, tiled=True),
        lax.all_gather(down_weight, "dp", axis=1, tiled=True),
    )
    cond_float = condition.astype(jnp.float32)
    act_cond, silu_back = jax.vjp(jax.nn.silu, cond_float)
    act_low = act_cond.astype(jnp.bfloat16)
    mod_half = jnp.dot(act_low, full_ada, preferred_element_type=jnp.float32)
    modulation_vectors = lax.all_gather(mod_half, "tensor", axis=1, tiled=True)
    token_wise = jnp.einsum(
        "jyq,jqu->jyu",
        choose_rows,
        modulation_vectors.reshape(sequence_count, number_of_images, 6 * hidden_width),
        precision=highest_precision,
    ).reshape(number_of_tokens, 6 * hidden_width)
    shift_one, scale_one, gate_one, shift_two, scale_two, gate_two = jnp.split(
        token_wise, 6, axis=1
    )
    hidden_float = hidden_in.astype(jnp.float32)
    modulated_one, norm_one_back = jax.vjp(modulate, hidden_float, shift_one, scale_one)
    xm_one = modulated_one.astype(jnp.bfloat16)
    attn_flat = full_attn.reshape(hidden_width, 4 * half_width)
    projected = jnp.dot(xm_one, attn_flat, preferred_element_type=jnp.float32).reshape(
        number_of_tokens, 4, half_width
    )
    queries = projected[:, 0].astype(jnp.bfloat16)
    keys_low = projected[:, 1].astype(jnp.bfloat16)
    values = projected[:, 2].astype(jnp.bfloat16)
    gate_raw = projected[:, 3]
    forget_raw = jnp.dot(xm_one, full_forget, preferred_element_type=jnp.float32) + forget_bias
    mixer_local = functools.partial(token_mixer, token_keys=token_keys, tap_list=tap_list)
    mixed_out, mixer_back = jax.vjp(
        mixer_local,
        queries.astype(jnp.float32),
        keys_low.astype(jnp.float32),
        values.astype(jnp.float32),
        gate_raw,
        forget_raw,
        conv_weight.astype(jnp.float32),
    )
    mixed_low = mixed_out.astype(jnp.bfloat16)
    attn_out = tensor_total(jnp.dot(mixed_low, full_out, preferred_element_type=jnp.float32))
    after_attn = hidden_float + gate_one * attn_out
    modulated_two, norm_two_back = jax.vjp(modulate, after_attn, shift_two, scale_two)
    xm_two = modulated_two.astype(jnp.bfloat16)
    up_value = jnp.dot(xm_two, full_up, preferred_element_type=jnp.float32)
    act_value, gelu_back = jax.vjp(gelu_tanh, up_value)
    act_ffn = act_value.astype(jnp.bfloat16)
    down_value = tensor_total(jnp.dot(act_ffn, full_down, preferred_element_type=jnp.float32))
    hidden_out = (after_attn + gate_two * down_value).astype(jnp.bfloat16)
    full_ada, full_attn, full_forget, full_out, full_up, full_down = (
        lax.all_gather(shards[0], "dp", axis=0, tiled=True),
        lax.all_gather(shards[1], "dp", axis=0, tiled=True),
        lax.all_gather(shards[2], "dp", axis=0, tiled=True),
        lax.all_gather(shards[3], "dp", axis=1, tiled=True),
        lax.all_gather(shards[4], "dp", axis=0, tiled=True),
        lax.all_gather(shards[5], "dp", axis=1, tiled=True),
    )
    attn_flat = full_attn.reshape(hidden_width, 4 * half_width)
    upstream = cotangent.astype(jnp.float32)
    delta_down = (gate_two * upstream).astype(jnp.bfloat16)
    delta_gate_two = upstream * down_value
    delta_act = jnp.einsum("nd,fd->nf", delta_down, full_down, preferred_element_type=jnp.float32)
    local_down_grad = jnp.einsum(
        "nf,nd->fd", act_ffn, delta_down, preferred_element_type=jnp.float32
    )
    delta_up = gelu_back(delta_act)[0].astype(jnp.bfloat16)
    local_up_grad = jnp.einsum("nd,nf->df", xm_two, delta_up, preferred_element_type=jnp.float32)
    delta_xm_two = tensor_total(
        jnp.einsum("nf,df->nd", delta_up, full_up, preferred_element_type=jnp.float32)
    )
    delta_after, delta_shift_two, delta_scale_two = norm_two_back(delta_xm_two)
    delta_after = delta_after + upstream
    delta_attn = (gate_one * delta_after).astype(jnp.bfloat16)
    delta_gate_one = delta_after * attn_out
    local_out_grad = jnp.einsum(
        "nc,nd->cd", mixed_low, delta_attn, preferred_element_type=jnp.float32
    )
    delta_mixed = jnp.einsum("nd,cd->nc", delta_attn, full_out, preferred_element_type=jnp.float32)
    delta_query, delta_key, delta_value, delta_gate, delta_forget, delta_conv = mixer_back(
        delta_mixed
    )
    delta_proj = (
        jnp.stack([delta_query, delta_key, delta_value, delta_gate], axis=1)
        .astype(jnp.bfloat16)
        .reshape(number_of_tokens, 4 * half_width)
    )
    local_attn_grad = jnp.einsum(
        "nd,nc->dc", xm_one, delta_proj, preferred_element_type=jnp.float32
    ).reshape(hidden_width, 4, half_width)
    xm_one_float = xm_one.astype(jnp.float32)
    local_forget_grad = jnp.einsum(
        "nd,nh->dh", xm_one_float, delta_forget, precision=highest_precision
    )
    partial_back = jnp.einsum(
        "nc,dc->nd", delta_proj, attn_flat, preferred_element_type=jnp.float32
    ) + jnp.einsum(
        "nh,dh->nd", delta_forget, full_forget.astype(jnp.float32), precision=highest_precision
    )
    delta_xm_one = tensor_total(partial_back)
    delta_input, delta_shift_one, delta_scale_one = norm_one_back(delta_xm_one)
    grad_hidden = (delta_after + delta_input).astype(jnp.bfloat16)
    side_index = lax.axis_index("tensor")
    first_group = jnp.concatenate([delta_shift_one, delta_scale_one, delta_gate_one], axis=1)
    second_group = jnp.concatenate([delta_shift_two, delta_scale_two, delta_gate_two], axis=1)
    delta_tokens = jnp.where(side_index == 0, first_group, second_group)
    delta_mod = (
        jnp.einsum(
            "mxz,mxk->mzk",
            choose_rows,
            delta_tokens.reshape(sequence_count, length, 3 * hidden_width),
            precision=highest_precision,
        )
        .reshape(sequence_count * number_of_images, 3 * hidden_width)
        .astype(jnp.bfloat16)
    )
    local_ada_grad = jnp.einsum("id,ie->de", act_low, delta_mod, preferred_element_type=jnp.float32)
    delta_cond = lax.psum(
        jnp.einsum("ie,de->id", delta_mod, full_ada, preferred_element_type=jnp.float32), "tensor"
    )
    grad_condition = silu_back(delta_cond)[0].astype(jnp.bfloat16)
    grad_conv, grad_bias = lax.psum((delta_conv, jnp.sum(delta_forget, axis=0)), "dp")
    grad_ada, grad_attn, grad_forget, grad_out_weight, grad_up, grad_down = (
        lax.psum_scatter(local_ada_grad, "dp", scatter_dimension=0, tiled=True),
        lax.psum_scatter(local_attn_grad, "dp", scatter_dimension=0, tiled=True),
        lax.psum_scatter(local_forget_grad, "dp", scatter_dimension=0, tiled=True),
        lax.psum_scatter(local_out_grad, "dp", scatter_dimension=1, tiled=True),
        lax.psum_scatter(local_up_grad, "dp", scatter_dimension=0, tiled=True),
        lax.psum_scatter(local_down_grad, "dp", scatter_dimension=1, tiled=True),
    )
    return (
        hidden_out,
        grad_hidden,
        grad_condition,
        grad_ada,
        grad_attn,
        grad_forget,
        grad_bias,
        grad_conv,
        grad_out_weight,
        grad_up,
        grad_down,
    )


def solution(mesh):
    in_specs = (
        P("dp", None),
        P("dp", None),
        P("dp", None),
        P("dp", None),
        P("dp", "tensor"),
        P("dp", None, "tensor"),
        P("dp", "tensor"),
        P("tensor"),
        P(None, "tensor"),
        P("tensor", "dp"),
        P("dp", "tensor"),
        P("tensor", "dp"),
        P("dp", None),
    )
    out_specs = (
        P("dp", None),
        P("dp", None),
        P("dp", None),
        P("dp", "tensor"),
        P("dp", None, "tensor"),
        P("dp", "tensor"),
        P("tensor"),
        P(None, "tensor"),
        P("tensor", "dp"),
        P("dp", "tensor"),
        P("tensor", "dp"),
    )
    return jax.shard_map(body, mesh=mesh, in_specs=in_specs, out_specs=out_specs, check_vma=False)
```

profile of v0, /device:TPU:0, one launch (start us, length us, event | category | flops | bytes accessed | tf_op | source)
XLA Modules:
  0.0 1326.6 jit_solution(6717316120422794878)
XLA Ops:
  13.2 23.5 %all-gather = bf16[16,72,8]{1,2,0:T(8,128)(2,1)S(1)} all-gather(bf16[1,72,8]{1,2,0:T(8,128)(2,1)S(1)} %bitcast.201), channel_id=1, replica_groups=mesh['dp'=16,'tensor'=2] {'dp'}, dimensions={0}, use_global_device_ids=true | all-gather | bytes 19584 | tf_op jit(solution)/shard_map/all_gather | solution.py:151
  45.3 27.8 %all-gather.13.cloned.1.call-done = bf16[1152,4,576]{2,0,1:T(8,128)(2,1)} async-done(((bf16[72,4,576]{2,0,1:T(8,128)(2,1)}), bf16[1152,4,576]{2,0,1:T(8,128)(2,1)}) %all-gather.13.cloned.1.call-update) | async-done | bytes 5308432 | tf_op jit(solution)/shard_map/all_gather | solution.py:150
  73.1 8.5 copy.425
  81.7 63.8 %all-gather.11.cloned.1.call-done = bf16[1152,3456]{1,0:T(8,128)(2,1)} async-done(((bf16[72,3456]{1,0:T(8,128)(2,1)}), bf16[1152,3456]{1,0:T(8,128)(2,1)}) %all-gather.11.cloned.1.call-update) | async-done | bytes 7962640 | tf_op jit(solution)/shard_map/all_gather | solution.py:149
  175.7 6.6 while.34
  239.7 20.6 %reduce-scatter.29.cloned.1.call-done = f32[576,256]{1,0:T(8,128)} async-done(((f32[1152,256]{1,0:T(8,128)}), f32[576,256]{1,0:T(8,128)}) %reduce-scatter.29.cloned.1.call-update) | async-done | bytes 589840
  262.2 22.3 %all-gather.17.cloned.1.call-done = f32[256,1152]{0,1:T(8,128)} async-done(((f32[256,576]{0,1:T(8,128)}), f32[256,1152]{0,1:T(8,128)}) %all-gather.17.cloned.1.call-update) | async-done | bytes 1179664 | tf_op jit(solution)/shard_map/all_gather | solution.py:66
  292.1 50.8 %all-gather.19.cloned.1.call-done = bf16[1152,2304]{1,0:T(8,128)(2,1)} async-done(((bf16[72,2304]{1,0:T(8,128)(2,1)}), bf16[1152,2304]{1,0:T(8,128)(2,1)}) %all-gather.19.cloned.1.call-update) | async-done | bytes 5308432 | tf_op jit(solution)/shard_map/all_gather | solution.py:153
  348.7 51.3 %all-gather.21.cloned.1.call-done = bf16[2304,1152]{0,1:T(8,128)(2,1)} async-done(((bf16[2304,72]{0,1:T(8,128)(2,1)}), bf16[2304,1152]{0,1:T(8,128)(2,1)}) %all-gather.21.cloned.1.call-update) | async-done | bytes 5308432 | tf_op jit(solution)/shard_map/all_gather | solution.py:154
  416.1 14.5 %reduce-scatter.33.cloned.1.call-done = f32[576,256]{1,0:T(8,128)} async-done(((f32[1152,256]{1,0:T(8,128)}), f32[576,256]{1,0:T(8,128)}) %reduce-scatter.33.cloned.1.call-update) | async-done | bytes 589840
  430.7 24.0 %reduce-scatter.31.cloned.1.call-done = f32[576,256]{1,0:T(8,128)} async-done(((f32[1152,256]{1,0:T(8,128)}), f32[576,256]{1,0:T(8,128)}) %reduce-scatter.31.cloned.1.call-update) | async-done | bytes 589840
  455.0 23.9 %all-gather.25.cloned.1.call-done = f32[256,1152]{0,1:T(8,128)} async-done(((f32[256,576]{0,1:T(8,128)}), f32[256,1152]{0,1:T(8,128)}) %all-gather.25.cloned.1.call-update) | async-done | bytes 1179664 | tf_op jit(solution)/shard_map/all_gather | solution.py:66
  483.5 19.7 %all-gather.23.cloned.1.call-done = f32[256,1152]{0,1:T(8,128)} async-done(((f32[256,576]{0,1:T(8,128)}), f32[256,1152]{0,1:T(8,128)}) %all-gather.23.cloned.1.call-update) | async-done | bytes 1179664 | tf_op jit(solution)/shard_map/all_gather | solution.py:66
  590.5 10.2 while.35
  646.3 21.9 %reduce-scatter.35.cloned.1.call-done = f32[576,256]{1,0:T(8,128)} async-done(((f32[1152,256]{1,0:T(8,128)}), f32[576,256]{1,0:T(8,128)}) %reduce-scatter.35.cloned.1.call-update) | async-done | bytes 589840
  686.0 7.6 fusion.137
  702.8 10.0 fusion.133
  717.7 67.2 %all-reduce.13 = (f32[1152,8]{0,1:T(8,128)S(1)}, f32[8]{0:T(128)}, f32[9,576]{1,0:T(8,128)}) all-reduce(f32[1152,8]{0,1:T(8,128)S(1)} %fusion.120, f32[8]{0:T(128)S(1)} %neg.58, f32[9,576]{1,0:T(8,128)S(1)} %pad_add_fusion), channel_id=8, replica_groups=mesh['dp'=16,'tensor'=2] {'dp'}, use_global_device_ids=true, to_apply=%region_43.45.clone | all-reduce | flops 14408 | bytes 115264
  791.0 7.7 psum.21
  799.3 28.3 %reduce-scatter.23.cloned.1.call-done = f32[72,4,576]{2,0,1:T(8,128)} async-done(((f32[1152,4,576]{2,0,1:T(8,128)}), f32[72,4,576]{2,0,1:T(8,128)}) %reduce-scatter.23.cloned.1.call-update) | async-done | bytes 663568 | tf_op jit(solution)/shard_map/reduce_scatter | solution.py:276
  829.9 65.6 %reduce-scatter.39.cloned.1.call-done = f32[576,72]{0,1:T(8,128)} async-done(((f32[576,1152]{0,1:T(8,128)}), f32[576,72]{0,1:T(8,128)}) %reduce-scatter.39.cloned.1.call-update) | async-done | bytes 165904
  895.5 124.2 %reduce-scatter.25.cloned.1.call-done = f32[72,2304]{1,0:T(8,128)} async-done(((f32[1152,2304]{1,0:T(8,128)}), f32[72,2304]{1,0:T(8,128)}) %reduce-scatter.25.cloned.1.call-update) | async-done | bytes 663568 | tf_op jit(solution)/shard_map/reduce_scatter | solution.py:279
  1019.7 124.8 %reduce-scatter.27.cloned.1.call-done = f32[2304,72]{0,1:T(8,128)} async-done(((f32[2304,1152]{0,1:T(8,128)}), f32[2304,72]{0,1:T(8,128)}) %reduce-scatter.27.cloned.1.call-update) | async-done | bytes 663568 | tf_op jit(solution)/shard_map/reduce_scatter | solution.py:280
  1144.5 174.8 %reduce-scatter.37.cloned.1.call-done = f32[72,3456]{1,0:T(8,128)} async-done(((f32[1152,3456]{1,0:T(8,128)}), f32[72,3456]{1,0:T(8,128)}) %reduce-scatter.37.cloned.1.call-update) | async-done | bytes 995344
  (557 shorter events, 325.7 us)
Async XLA Ops:
  7.2 65.8 %all-gather.13.cloned.1.call-start = ((), (), s32[]{:S(2)}) async-start(), calls=%async_computation.10 | async-start | bytes 6266880 | tf_op jit(solution)/shard_map/all_gather | solution.py:150
  9.1 136.4 %all-gather.11.cloned.1.call-start = ((), (), s32[]{:S(2)}) async-start(), calls=%async_computation.9 | async-start | bytes 8460288 | tf_op jit(solution)/shard_map/all_gather | solution.py:149
  9.9 226.7 %all-gather.15.cloned.1.call-start = ((), (), s32[]{:S(2)}) async-start(), calls=%async_computation.11 | async-start | bytes 1566720 | tf_op jit(solution)/shard_map/all_gather | solution.py:152
  10.6 249.8 %reduce-scatter.29.cloned.1.call-start = ((), (), s32[]{:S(2)}) async-start(), calls=%async_computation.21 | async-start | bytes 1769472
  10.9 144.8 %copy-start.71 = (s32[256]{0:T(256)}, s32[256]{0:T(256)S(1)}, u32[]{:S(2)}) copy-start(s32[256]{0:T(256)S(1)} %fusion.123) | copy-start | bytes 3076
  12.8 145.9 %copy-start.89 = (f32[256]{0:T(256)}, f32[256]{0:T(256)S(1)}, u32[]{:S(2)}) copy-start(f32[256]{0:T(256)S(1)} %broadcast_multiply_fusion.1) | copy-start | bytes 3076
  13.1 145.6 %copy-start.103 = (f32[256]{0:T(256)}, f32[256]{0:T(256)S(1)}, u32[]{:S(2)}) copy-start(f32[256]{0:T(256)S(1)} %fusion.125) | copy-start | bytes 3076
  36.7 125.2 %copy-start.61 = (bf16[1152,8]{0,1:T(8,128)(2,1)}, bf16[1152,8]{0,1:T(8,128)(2,1)S(1)}, u32[]{:S(2)}) copy-start(bf16[1152,8]{0,1:T(8,128)(2,1)S(1)} %reshape.1109) | copy-start | bytes 55300
  172.3 406.8 %copy-start.63 = (f32[4,64,8]{1,2,0:T(8,128)}, f32[4,64,8]{1,2,0:T(8,128)S(1)}, u32[]{:S(2)}) copy-start(f32[4,64,8]{1,2,0:T(8,128)S(1)} %get-tuple-element.444) | copy-start | bytes 24580
  172.3 432.6 %copy-start.65 = (f32[4,64,8]{1,2,0:T(8,128)}, f32[4,64,8]{1,2,0:T(8,128)S(1)}, u32[]{:S(2)}) copy-start(f32[4,64,8]{1,2,0:T(8,128)S(1)} %get-tuple-element.445) | copy-start | bytes 24580
  239.7 44.8 %all-gather.17.cloned.1.call-start = ((), (), s32[]{:S(2)}) async-start(), calls=%async_computation.12 | async-start | bytes 1769472 | tf_op jit(solution)/shard_map/all_gather | solution.py:66
  260.4 82.5 %all-gather.19.cloned.1.call-start = ((), (), s32[]{:S(2)}) async-start(), calls=%async_computation.13 | async-start | bytes 5640192 | tf_op jit(solution)/shard_map/all_gather | solution.py:153
  261.0 139.1 %all-gather.21.cloned.1.call-start = ((), (), s32[]{:S(2)}) async-start(), calls=%async_computation.14 | async-start | bytes 5640192 | tf_op jit(solution)/shard_map/all_gather | solution.py:154
  261.7 168.9 %reduce-scatter.33.cloned.1.call-start = ((), (), s32[]{:S(2)}) async-start(), calls=%async_computation.23 | async-start | bytes 1769472
  410.0 44.7 %reduce-scatter.31.cloned.1.call-start = ((), (), s32[]{:S(2)}) async-start(), calls=%async_computation.22 | async-start | bytes 1769472
  416.1 62.8 %all-gather.25.cloned.1.call-start = ((), (), s32[]{:S(2)}) async-start(), calls=%async_computation.16 | async-start | bytes 1769472 | tf_op jit(solution)/shard_map/all_gather | solution.py:66
  430.7 72.6 %all-gather.23.cloned.1.call-start = ((), (), s32[]{:S(2)}) async-start(), calls=%async_computation.15 | async-start | bytes 1769472 | tf_op jit(solution)/shard_map/all_gather | solution.py:66
  454.8 213.4 %reduce-scatter.35.cloned.1.call-start = ((), (), s32[]{:S(2)}) async-start(), calls=%async_computation.24 | async-start | bytes 1769472
  646.2 47.6 %all-gather.27.cloned.1.call-start = ((), (), s32[]{:S(2)}) async-start(), calls=%async_computation.17 | async-start | bytes 1769472 | tf_op jit(solution)/shard_map/all_gather | solution.py:66
  668.2 159.5 %reduce-scatter.23.cloned.1.call-start = ((), (), s32[]{:S(2)}) async-start(), calls=%async_computation.18 | async-start | bytes 12533760 | tf_op jit(solution)/shard_map/reduce_scatter | solution.py:276
  674.5 221.0 %reduce-scatter.39.cloned.1.call-start = ((), (), s32[]{:S(2)}) async-start(), calls=%async_computation.26 | async-start | bytes 3133440
  677.9 341.8 %reduce-scatter.25.cloned.1.call-start = ((), (), s32[]{:S(2)}) async-start(), calls=%async_computation.19 | async-start | bytes 11280384 | tf_op jit(solution)/shard_map/reduce_scatter | solution.py:279
  685.0 459.5 %reduce-scatter.27.cloned.1.call-start = ((), (), s32[]{:S(2)}) async-start(), calls=%async_computation.20 | async-start | bytes 11280384 | tf_op jit(solution)/shard_map/reduce_scatter | solution.py:280
  693.7 625.6 %reduce-scatter.37.cloned.1.call-start = ((), (), s32[]{:S(2)}) async-start(), calls=%async_computation.25 | async-start | bytes 16920576
  (139 other events, 1033.5 us)
Sparse Core Ops, SparseCore 0:
  10.8 62.2 all-gather.12
  75.2 70.2 all-gather.10
  147.6 37.8 all-gather.14
  239.8 20.4 reduce-scatter.28
  261.7 22.7 all-gather.16
  286.6 56.2 all-gather.18
  345.1 54.9 all-gather.20
  410.2 20.4 reduce-scatter.32
  432.9 21.8 reduce-scatter.30
  456.1 22.7 all-gather.24
  480.5 22.7 all-gather.22
  646.3 21.8 reduce-scatter.34
  669.7 22.7 all-gather.26
  696.5 131.1 reduce-scatter.22
  832.0 63.3 reduce-scatter.38
  900.0 119.7 reduce-scatter.24
  1024.2 120.2 reduce-scatter.26
  1149.1 170.1 reduce-scatter.36
where the time goes:
time: 1340 us; the launch traced here: 1330 us
  waiting for transfers between devices  862 us (64%)
  local copies, waits for them, and re-layouts  123 us (9%)
  matrix products  123 us (9%)
  blocking collectives  104 us (8%)
  other arithmetic  95.5 us (7%)
  between operations  17.5 us (1%)
    unnamed x24, waiting for transfers between devices  324 us
    reduce_scatter x1, waiting for transfers between devices, body(): lax.psum_scatter(local_down_grad, 'dp', scatter_dimension=1, tiled=True)  125 us
    reduce_scatter x1, waiting for transfers between devices, body(): lax.psum_scatter(local_up_grad, 'dp', scatter_dimension=0, tiled=True)  124 us
    unnamed x1, blocking collectives  67.2 us
    all_gather x4, waiting for transfers between devices, tensor_total(): return lax.all_gather(summed_half, 'tensor', axis=1, tiled=True)  66 us
    all_gather x1, waiting for transfers between devices, body(): lax.all_gather(ada_weight, 'dp', axis=0, tiled=True)  63.8 us
    all_gather x1, waiting for transfers between devices, body(): lax.all_gather(down_weight, 'dp', axis=1, tiled=True)  51.3 us
    all_gather x1, waiting for transfers between devices, body(): lax.all_gather(up_weight, 'dp', axis=0, tiled=True)  50.8 us
  transfers between devices with their start and end apart: 18, of which 16 were waited for; matrix products, arithmetic and copies ran while one was open for 13% of the time, Pallas kernels for 0%

commit v1 on v0

--- a/solution.py
+++ b/solution.py
@@ -9,6 +9,37 @@
 norm_epsilon = 1e-06
 head_epsilon = 1e-05
 highest_precision = lax.Precision.HIGHEST
+
+
+def samples_manage(incoming_x, dim_at):
+    oldest = list(incoming_x.shape[1:])
+    oldest[dim_at] *= incoming_x.shape[0]
+    y1 = jnp.moveaxis(incoming_x, 0, dim_at).reshape(oldest)
+    return y1
+
+
+def _point_ratios(matrix, device_axis, in_dim):
+    width = lax.axis_size(device_axis)
+    rack = [(k, (k + 1) % width) for k in range(width)]
+    grid = [(pp, q) for q, pp in rack]
+    latest, row_out = ([], [])
+    for t in range(width - 1):
+        if t % 2 == 0:
+            z2 = lax.ppermute(latest[-1] if latest else matrix, axis_name=device_axis, perm=rack)
+            latest.append(z2)
+        else:
+            row_out.append(
+                lax.ppermute(row_out[-1] if row_out else matrix, axis_name=device_axis, perm=grid)
+            )
+    odd = jnp.stack([*latest[::-1], matrix, *row_out], axis=0)
+    found_now = lax.axis_index(device_axis)
+    response = found_now - len(latest)
+    odd = odd[(jnp.arange(width) - response) % width]
+    y = samples_manage(odd, in_dim)
+    return y
+
+
+create_view = functools.partial(_point_ratios, device_axis="dp", in_dim=0)
 
 
 def layout(heights, widths, length):
@@ -150,7 +181,7 @@
         lax.all_gather(attn_weight, "dp", axis=0, tiled=True),
         lax.all_gather(forget_weight, "dp", axis=0, tiled=True),
         lax.all_gather(out_weight, "dp", axis=1, tiled=True),
-        lax.all_gather(up_weight, "dp", axis=0, tiled=True),
+        create_view(up_weight),
         lax.all_gather(down_weight, "dp", axis=1, tiled=True),
     )
     cond_float = condition.astype(jnp.float32)

time: 1340 us -> 1350 us (level)
  waiting for transfers between devices: 862 us -> 822 us
  starting transfers between devices: 1.61 us -> 33.4 us
  local copies, waits for them, and re-layouts: 123 us -> 146 us
    ppermute x0 -> x15, waiting for transfers between devices: none -> 51.5 us  [the longest x8 29 us: _point_ratios(): lax.ppermute(latest[-1] if latest else matrix, axis_name=device_axis, per...]
    all_gather x1, waiting for transfers between devices: 51.3 us -> 0.01 us  [body(): lax.all_gather(down_weight, 'dp', axis=1, tiled=True)]
    ppermute x0 -> x15, starting transfers between devices: none -> 32.2 us  [the longest x7 32.1 us: _point_ratios(): lax.ppermute(row_out[-1] if row_out else matrix, axis_name=device_axis, p...]
    all_gather x4, waiting for transfers between devices: 66 us -> 43.6 us  [tensor_total(): return lax.all_gather(summed_half, 'tensor', axis=1, tiled=True)]
    all_gather x1, waiting for transfers between devices: 50.8 us -> 33.5 us  [body(): lax.all_gather(shards[4], 'dp', axis=0, tiled=True)]
    unnamed x295 -> x324, local copies, waits for them, and re-layouts: 17.8 us -> 34.2 us
  transfers between devices with their start and end apart: 18 -> 33, of which waited for: 16 -> 26; matrix products, arithmetic and copies ran while one was open for 13% -> 15% of each run, Pallas kernels for 0% -> 0%
where the time goes in v1:
time: 1350 us; the launch traced here: 1340 us
  waiting for transfers between devices  822 us (61%)
  local copies, waits for them, and re-layouts  146 us (11%)
  matrix products  125 us (9%)
  blocking collectives  104 us (8%)
  other arithmetic  94.5 us (7%)
  starting transfers between devices  33.4 us (2%)
  between operations  17.5 us (1%)
    unnamed x24, waiting for transfers between devices  324 us
    reduce_scatter x1, waiting for transfers between devices, body(): lax.psum_scatter(local_down_grad, 'dp', scatter_dimension=1, tiled=True)  125 us
    reduce_scatter x1, waiting for transfers between devices, body(): lax.psum_scatter(local_up_grad, 'dp', scatter_dimension=0, tiled=True)  124 us
    unnamed x1, blocking collectives  67.1 us
    all_gather x1, waiting for transfers between devices, body(): lax.all_gather(ada_weight, 'dp', axis=0, tiled=True)  63.9 us
    all_gather x4, waiting for transfers between devices, tensor_total(): return lax.all_gather(summed_half, 'tensor', axis=1, tiled=True)  43.6 us
    unnamed x324, local copies, waits for them, and re-layouts  34.2 us
    all_gather x1, waiting for transfers between devices, body(): lax.all_gather(shards[4], 'dp', axis=0, tiled=True)  33.5 us
  transfers between devices with their start and end apart: 33, of which 26 were waited for; matrix products, arithmetic and copies ran while one was open for 15% of the time, Pallas kernels for 0%

profile of v1, /device:TPU:0, one launch (start us, length us, event | category | flops | bytes accessed | tf_op | source)
XLA Modules:
  0.0 1342.8 jit_solution(14442718153704420574)
XLA Ops:
  13.1 23.5 %all-gather = bf16[16,72,8]{1,2,0:T(8,128)(2,1)S(1)} all-gather(bf16[1,72,8]{1,2,0:T(8,128)(2,1)S(1)} %bitcast.237), channel_id=1, replica_groups=mesh['dp'=16,'tensor'=2] {'dp'}, dimensions={0}, use_global_device_ids=true | all-gather | bytes 19584 | tf_op jit(solution)/shard_map/all_gather | solution.py:182
  44.7 28.4 %all-gather.13.cloned.1.call-done = bf16[1152,4,576]{2,0,1:T(8,128)(2,1)} async-done(((bf16[72,4,576]{2,0,1:T(8,128)(2,1)}), bf16[1152,4,576]{2,0,1:T(8,128)(2,1)}) %all-gather.13.cloned.1.call-update) | async-done | bytes 5308432 | tf_op jit(solution)/shard_map/all_gather | solution.py:181
  73.1 8.5 copy.425
  81.6 63.9 %all-gather.11.cloned.1.call-done = bf16[1152,3456]{1,0:T(8,128)(2,1)} async-done(((bf16[72,3456]{1,0:T(8,128)(2,1)}), bf16[1152,3456]{1,0:T(8,128)(2,1)}) %all-gather.11.cloned.1.call-update) | async-done | bytes 7962640 | tf_op jit(solution)/shard_map/all_gather | solution.py:180
  240.0 20.6 %reduce-scatter.29.cloned.1.call-done = f32[576,256]{1,0:T(8,128)} async-done(((f32[1152,256]{1,0:T(8,128)}), f32[576,256]{1,0:T(8,128)}) %reduce-scatter.29.cloned.1.call-update) | async-done | bytes 589840
  261.4 9.2 collective-permute-done
  319.8 10.3 collective-permute-done.12
  378.8 7.3 fusion.21
  386.1 33.5 %all-gather.23.cloned.1.call-done = bf16[1152,2304]{1,0:T(8,128)(2,1)} async-done(((bf16[72,2304]{1,0:T(8,128)(2,1)}), bf16[1152,2304]{1,0:T(8,128)(2,1)}) %all-gather.23.cloned.1.call-update) | async-done | bytes 5308432 | tf_op jit(solution)/shard_map/all_gather | solution.py:238
  431.1 14.6 %reduce-scatter.33.cloned.1.call-done = f32[576,256]{1,0:T(8,128)} async-done(((f32[1152,256]{1,0:T(8,128)}), f32[576,256]{1,0:T(8,128)}) %reduce-scatter.33.cloned.1.call-update) | async-done | bytes 589840
  445.7 24.0 %reduce-scatter.31.cloned.1.call-done = f32[576,256]{1,0:T(8,128)} async-done(((f32[1152,256]{1,0:T(8,128)}), f32[576,256]{1,0:T(8,128)}) %reduce-scatter.31.cloned.1.call-update) | async-done | bytes 589840
  470.1 23.9 %all-gather.25.cloned.1.call-done = f32[256,1152]{0,1:T(8,128)} async-done(((f32[256,576]{0,1:T(8,128)}), f32[256,1152]{0,1:T(8,128)}) %all-gather.25.cloned.1.call-update) | async-done | bytes 1179664 | tf_op jit(solution)/shard_map/all_gather | solution.py:97
  498.6 19.7 %all-gather.21.cloned.1.call-done = f32[256,1152]{0,1:T(8,128)} async-done(((f32[256,576]{0,1:T(8,128)}), f32[256,1152]{0,1:T(8,128)}) %all-gather.21.cloned.1.call-update) | async-done | bytes 1179664 | tf_op jit(solution)/shard_map/all_gather | solution.py:97
  606.4 10.4 while.35
  662.4 21.9 %reduce-scatter.35.cloned.1.call-done = f32[576,256]{1,0:T(8,128)} async-done(((f32[1152,256]{1,0:T(8,128)}), f32[576,256]{1,0:T(8,128)}) %reduce-scatter.35.cloned.1.call-update) | async-done | bytes 589840
  702.2 7.6 fusion.139
  718.9 10.0 fusion.135
  733.8 67.1 %all-reduce.13 = (f32[1152,8]{0,1:T(8,128)S(1)}, f32[8]{0:T(128)}, f32[9,576]{1,0:T(8,128)}) all-reduce(f32[1152,8]{0,1:T(8,128)S(1)} %fusion.120, f32[8]{0:T(128)S(1)} %neg.58, f32[9,576]{1,0:T(8,128)S(1)} %pad_add_fusion), channel_id=8, replica_groups=mesh['dp'=16,'tensor'=2] {'dp'}, use_global_device_ids=true, to_apply=%region_43.45.clone | all-reduce | flops 14408 | bytes 115264
  807.0 7.9 psum.21
  815.5 28.3 %reduce-scatter.23.cloned.1.call-done = f32[72,4,576]{2,0,1:T(8,128)} async-done(((f32[1152,4,576]{2,0,1:T(8,128)}), f32[72,4,576]{2,0,1:T(8,128)}) %reduce-scatter.23.cloned.1.call-update) | async-done | bytes 663568 | tf_op jit(solution)/shard_map/reduce_scatter | solution.py:307
  846.0 65.6 %reduce-scatter.39.cloned.1.call-done = f32[576,72]{0,1:T(8,128)} async-done(((f32[576,1152]{0,1:T(8,128)}), f32[576,72]{0,1:T(8,128)}) %reduce-scatter.39.cloned.1.call-update) | async-done | bytes 165904
  911.6 124.2 %reduce-scatter.25.cloned.1.call-done = f32[72,2304]{1,0:T(8,128)} async-done(((f32[1152,2304]{1,0:T(8,128)}), f32[72,2304]{1,0:T(8,128)}) %reduce-scatter.25.cloned.1.call-update) | async-done | bytes 663568 | tf_op jit(solution)/shard_map/reduce_scatter | solution.py:310
  1035.9 124.8 %reduce-scatter.27.cloned.1.call-done = f32[2304,72]{0,1:T(8,128)} async-done(((f32[2304,1152]{0,1:T(8,128)}), f32[2304,72]{0,1:T(8,128)}) %reduce-scatter.27.cloned.1.call-update) | async-done | bytes 663568 | tf_op jit(solution)/shard_map/reduce_scatter | solution.py:311
  1160.7 174.8 %reduce-scatter.37.cloned.1.call-done = f32[72,3456]{1,0:T(8,128)} async-done(((f32[1152,3456]{1,0:T(8,128)}), f32[72,3456]{1,0:T(8,128)}) %reduce-scatter.37.cloned.1.call-update) | async-done | bytes 995344
  (619 shorter events, 412.0 us)
Async XLA Ops:
  7.2 65.9 %all-gather.13.cloned.1.call-start = ((), (), s32[]{:S(2)}) async-start(), calls=%async_computation.10 | async-start | bytes 6266880 | tf_op jit(solution)/shard_map/all_gather | solution.py:181
  9.1 136.4 %all-gather.11.cloned.1.call-start = ((), (), s32[]{:S(2)}) async-start(), calls=%async_computation.9 | async-start | bytes 8460288 | tf_op jit(solution)/shard_map/all_gather | solution.py:180
  9.9 227.0 %all-gather.15.cloned.1.call-start = ((), (), s32[]{:S(2)}) async-start(), calls=%async_computation.11 | async-start | bytes 1566720 | tf_op jit(solution)/shard_map/all_gather | solution.py:183
  10.6 250.0 %reduce-scatter.29.cloned.1.call-start = ((), (), s32[]{:S(2)}) async-start(), calls=%async_computation.21 | async-start | bytes 1769472
  240.0 127.9 %all-gather.17.cloned.1.call-start = ((), (), s32[]{:S(2)}) async-start(), calls=%async_computation.12 | async-start | bytes 1769472 | tf_op jit(solution)/shard_map/all_gather | solution.py:97
  260.7 118.1 %all-gather.19.cloned.1.call-start = ((), (), s32[]{:S(2)}) async-start(), calls=%async_computation.13 | async-start | bytes 5640192 | tf_op jit(solution)/shard_map/all_gather | solution.py:185
  261.2 158.3 %all-gather.23.cloned.1.call-start = ((), (), s32[]{:S(2)}) async-start(), calls=%async_computation.15 | async-start | bytes 5640192 | tf_op jit(solution)/shard_map/all_gather | solution.py:238
  289.2 14.5 %collective-permute-start.10 = (bf16[72,2304]{1,0:T(8,128)(2,1)S(1)}, bf16[72,2304]{1,0:T(8,128)(2,1)S(1)}, u32[]{:S(2)}, u32[]{:S(2)}) collective-permute-start(bf16[72,2304]{1,0:T(8,128)(2,1)S(1)} %collective-permute-done.9), channel_id=1, source_target_pairs={{2,0},{4,2},{6,4},{8,6},{10,8},{12,10},{14,12},{16,14},{18,16},{20... | collective-permute-start | bytes 995336 | tf_op jit(solution)/shard_map/ppermute | solution.py:32
  298.5 12.0 collective-permute-start.4
  314.0 16.2 %collective-permute-start.12 = (bf16[72,2304]{1,0:T(8,128)(2,1)S(1)}, bf16[72,2304]{1,0:T(8,128)(2,1)}, u32[]{:S(2)}, u32[]{:S(2)}) collective-permute-start(bf16[72,2304]{1,0:T(8,128)(2,1)S(1)} %collective-permute-done.11), channel_id=1, source_target_pairs={{2,0},{4,2},{6,4},{8,6},{10,8},{12,10},{14,12},{16,14},{18,16},{20... | collective-permute-start | bytes 995336 | tf_op jit(solution)/shard_map/ppermute | solution.py:32
  319.8 16.5 %collective-permute-start.6 = (bf16[72,2304]{1,0:T(8,128)(2,1)S(1)}, bf16[72,2304]{1,0:T(8,128)(2,1)}, u32[]{:S(2)}, u32[]{:S(2)}) collective-permute-start(bf16[72,2304]{1,0:T(8,128)(2,1)S(1)} %collective-permute-done.5), channel_id=1, source_target_pairs={{0,2},{2,4},{4,6},{6,8},{8,10},{10,12},{12,14},{14,16},{16,18},{18... | collective-permute-start | bytes 995336 | tf_op jit(solution)/shard_map/ppermute | solution.py:28
  330.1 10.6 collective-permute-start.13
  336.3 109.4 %reduce-scatter.33.cloned.1.call-start = ((), (), s32[]{:S(2)}) async-start(), calls=%async_computation.23 | async-start | bytes 1769472
  340.7 20.6 %collective-permute-start.14 = (bf16[72,2304]{1,0:T(8,128)(2,1)}, bf16[72,2304]{1,0:T(8,128)(2,1)S(1)}, u32[]{:S(2)}, u32[]{:S(2)}) collective-permute-start(bf16[72,2304]{1,0:T(8,128)(2,1)} %collective-permute-done.13), channel_id=1, source_target_pairs={{2,0},{4,2},{6,4},{8,6},{10,8},{12,10},{14,12},{16,14},{18,16},{20... | collective-permute-start | bytes 995336 | tf_op jit(solution)/shard_map/ppermute | solution.py:32
  425.1 44.7 %reduce-scatter.31.cloned.1.call-start = ((), (), s32[]{:S(2)}) async-start(), calls=%async_computation.22 | async-start | bytes 1769472
  431.1 62.9 %all-gather.25.cloned.1.call-start = ((), (), s32[]{:S(2)}) async-start(), calls=%async_computation.16 | async-start | bytes 1769472 | tf_op jit(solution)/shard_map/all_gather | solution.py:97
  445.7 72.6 %all-gather.21.cloned.1.call-start = ((), (), s32[]{:S(2)}) async-start(), calls=%async_computation.14 | async-start | bytes 1769472 | tf_op jit(solution)/shard_map/all_gather | solution.py:97
  469.8 214.6 %reduce-scatter.35.cloned.1.call-start = ((), (), s32[]{:S(2)}) async-start(), calls=%async_computation.24 | async-start | bytes 1769472
  662.4 47.5 %all-gather.27.cloned.1.call-start = ((), (), s32[]{:S(2)}) async-start(), calls=%async_computation.17 | async-start | bytes 1769472 | tf_op jit(solution)/shard_map/all_gather | solution.py:97
  684.4 159.5 %reduce-scatter.23.cloned.1.call-start = ((), (), s32[]{:S(2)}) async-start(), calls=%async_computation.18 | async-start | bytes 12533760 | tf_op jit(solution)/shard_map/reduce_scatter | solution.py:307
  690.6 221.0 %reduce-scatter.39.cloned.1.call-start = ((), (), s32[]{:S(2)}) async-start(), calls=%async_computation.26 | async-start | bytes 3133440
  694.1 341.8 %reduce-scatter.25.cloned.1.call-start = ((), (), s32[]{:S(2)}) async-start(), calls=%async_computation.19 | async-start | bytes 11280384 | tf_op jit(solution)/shard_map/reduce_scatter | solution.py:310
  701.1 459.6 %reduce-scatter.27.cloned.1.call-start = ((), (), s32[]{:S(2)}) async-start(), calls=%async_computation.20 | async-start | bytes 11280384 | tf_op jit(solution)/shard_map/reduce_scatter | solution.py:311
  709.8 625.7 %reduce-scatter.37.cloned.1.call-start = ((), (), s32[]{:S(2)}) async-start(), calls=%async_computation.25 | async-start | bytes 16920576
  (161 other events, 1872.4 us)
Sparse Core Ops, SparseCore 0:
  10.8 62.2 all-gather.12
  75.3 70.2 all-gather.10
  147.7 37.7 all-gather.14
  240.1 20.4 reduce-scatter.28
  262.0 22.7 all-gather.16
  286.9 70.7 all-gather.18
  359.9 59.6 all-gather.22
  425.2 20.4 reduce-scatter.32
  447.9 21.8 reduce-scatter.30
  471.2 22.7 all-gather.24
  495.5 22.7 all-gather.20
  662.5 21.8 reduce-scatter.34
  685.9 22.7 all-gather.26
  712.7 131.1 reduce-scatter.22
  848.2 63.4 reduce-scatter.38
  916.1 119.7 reduce-scatter.24
  1040.3 120.2 reduce-scatter.26
  1165.2 170.2 reduce-scatter.36
